TPU v7x, 32 devices: a whole 2x2x4 slice. The times are simulated.
32 devices in a mesh: prow: 4 (over y, x), pcol: 8 (over z, core).
Axes of the slice: x: 2, y: 2, z: 4, core: 2. Of those that a mesh axis runs over, the one named last changes fastest.
Arguments:
- matrix: float32 [16, 4, 256, 8, 8, 256], P(None, 'prow', None, None, 'pcol'), may hold values from -6 to 6, as said below
- factor: float32 [16, 4, 256, 8, 8, 256], P(None, 'prow', None, None, 'pcol'), may hold values from -3 to 3, as said below
Outputs:
- reduced: float32 [16, 4, 256, 8, 8, 256], P(None, 'prow', None, None, 'pcol')
Inputs may be any that keep to these rules, and one draw needn't show every extreme that they name: Symmetric matrix stored in its lower triangle: every entry above the diagonal is zero. `factor`: lower triangular with diagonal entries between 1 and 3; every entry above the diagonal is zero.
All inputs are finite; a program needn't handle non-finite values.
Results may differ from a plain program's by a relative error of at most 0.0001.
Values sent between devices are 32-bit elements; how exact they have to be, the bound alone decides.
A program may use at most 256 MiB of HBM per device.

v0:
```python
import jax
import jax.numpy as jnp
from jax import lax
from jax.sharding import PartitionSpec as P

BLOCKS = 2
highest = lax.Precision.HIGHEST


def spread(block, axis, source):
    block = jnp.where(lax.axis_index(axis) == source, block, jnp.zeros_like(block))
    return lax.psum(block, axis)


def product(left, right):
    return jnp.dot(left, right, precision=highest, preferred_element_type=jnp.float32)


def product_trans(left, right):
    return lax.dot_general(
        left, right, (((1,), (1,)), ((), ())), precision=highest, preferred_element_type=jnp.float32
    )


def diagonal_core(diag_block, diag_factor, width):
    identity = jnp.eye(width, dtype=jnp.float32)
    inverse = lax.linalg.triangular_solve(diag_factor, identity, left_side=True, lower=True)
    symmetric = diag_block + diag_block.T - jnp.diag(jnp.diagonal(diag_block))
    inner = product_trans(product(inverse, symmetric), inverse)
    return (inverse, 0.5 * (inner + inner.T))


def on_device(matrix, factor):
    row_tiles = matrix.shape[0]
    width = matrix.shape[2]
    col_tiles = matrix.shape[3]
    prow_count = lax.axis_size("prow")
    pcol_count = lax.axis_size("pcol")
    prow_index = lax.axis_index("prow")
    pcol_index = lax.axis_index("pcol")
    height = row_tiles * width
    local = matrix.reshape(height, col_tiles * width)
    factor_local = factor.reshape(height, col_tiles * width)
    tile_rows = jnp.arange(row_tiles, dtype=jnp.int32) * prow_count + prow_index
    tile_cols = jnp.arange(col_tiles, dtype=jnp.int32) * pcol_count + pcol_index
    offsets = jnp.arange(width, dtype=jnp.int32)
    elem_rows = (tile_rows[:, None] * width + offsets[None, :]).reshape(height)
    elem_cols = (tile_cols[:, None] * width + offsets[None, :]).reshape(col_tiles * width)
    lower_part = elem_rows[:, None] >= elem_cols[None, :]
    row_tile_of = jnp.repeat(tile_rows, width)[:, None]
    ratio = pcol_count // prow_count
    home = pcol_index % prow_count

    def select_columns(block):
        shaped = block.reshape(col_tiles, ratio, width, width)
        picked = lax.dynamic_index_in_dim(shaped, pcol_index // prow_count, 1, keepdims=False)
        return picked.reshape(col_tiles * width, width)

    for step in range(BLOCKS):
        owner_row = step % prow_count
        owner_col = step % pcol_count
        first = step // pcol_count * width
        diag_start = step // prow_count * width
        panel = local[:, first : first + width]
        factor_panel = factor_local[:, first : first + width]
        diag_block, diag_factor = (
            spread(panel[diag_start : diag_start + width], "prow", owner_row),
            spread(factor_panel[diag_start : diag_start + width], "prow", owner_row),
        )
        inverse, core = diagonal_core(diag_block, diag_factor, width)
        below = row_tile_of > step
        factor_rows = jnp.where(below, factor_panel, 0.0)
        shared = product(factor_rows, core)
        halfway = jnp.where(below, product_trans(panel, inverse), 0.0) - 0.5 * shared
        finished = halfway - 0.5 * shared
        got_half, got_factor = (
            spread(halfway, "pcol", owner_col),
            spread(factor_rows, "pcol", owner_col),
        )
        keeper = prow_index == home
        col_half, col_factor = lax.psum(
            (
                jnp.where(keeper, select_columns(got_half), 0.0),
                jnp.where(keeper, select_columns(got_factor), 0.0),
            ),
            "prow",
        )
        update = product_trans(
            jnp.concatenate([got_half, got_factor], 1), jnp.concatenate([col_factor, col_half], 1)
        )
        local = local - jnp.where(lower_part, update, 0.0)
        current = local[:, first : first + width]
        diag_rows = jnp.tile(jnp.tril(core), (row_tiles, 1))
        column = jnp.where(row_tile_of == step, diag_rows, jnp.where(below, finished, current))
        column = jnp.where(pcol_index == owner_col, column, current)
        local = local.at[:, first : first + width].set(column)
    return local.reshape(row_tiles, 1, width, col_tiles, 1, width)


def solution(mesh):
    placed = (P(None, "prow", None, None, "pcol", None), P(None, "prow", None, None, "pcol", None))
    return jax.shard_map(
        on_device,
        mesh=mesh,
        in_specs=placed,
        out_specs=P(None, "prow", None, None, "pcol", None),
        check_vma=False,
    )
```

profile of v0, /device:TPU:0, one launch (start us, length us, event | category | flops | bytes accessed | tf_op | source)
XLA Modules:
  0.0 1339.8 jit_solution(16150928784970390900)
XLA Ops:
  6.5 94.1 %reduce.10 = f32[16,256,8,256]{3,2,1,0:T(8,128)} reduce(f32[16,1,256,8,1,256]{5,4,3,2,1,0:T(1,128)} %param.8, f32[]{:T(128)} %constant.182), dimensions={1,4}, to_apply=%param.8.reduce_sub_computation | reduce | bytes 67108864 | tf_op args[0]
  100.6 29.9 %copy.42 = f32[512,8,8,256]{3,1,2,0:T(8,128)} copy(f32[512,8,8,256]{3,2,1,0:T(8,128)} %bitcast.119) | data formatting | bytes 67108864
  130.5 31.1 %copy.36 = f32[4096,2048]{0,1:T(8,128)} copy(f32[4096,2048]{1,0:T(8,128)} %bitcast.120) | data formatting | bytes 67108864 | tf_op jit(solution)/shard_map/reshape | solution.py:42
  161.6 93.3 %reduce.9 = f32[16,256,8,256]{3,2,1,0:T(8,128)} reduce(f32[16,1,256,8,1,256]{5,4,3,2,1,0:T(1,128)} %param.9, f32[]{:T(128)} %constant.182), dimensions={1,4}, to_apply=%param.9.reduce_sub_computation | reduce | bytes 67108864 | tf_op args[1]
  254.9 29.9 %copy.45 = f32[512,8,8,256]{3,1,2,0:T(8,128)} copy(f32[512,8,8,256]{3,2,1,0:T(8,128)} %bitcast.118) | data formatting | bytes 67108864
  305.4 30.7 %all-reduce.23.cloned.1.call-done = (f32[256,256]{0,1:T(8,128)}, f32[256,256]{0,1:T(8,128)}) async-done(((f32[256,256]{0,1:T(8,128)}, f32[256,256]{0,1:T(8,128)}), (f32[256,256]{0,1:T(8,128)}, f32[256,256]{0,1:T(8,128)})) %all-reduce.23.cloned.1.call-update) | async-done | bytes 524304 | tf_op jit(solution)/shard_map/psum | solution.py:12
  342.5 19.7 %custom-call.8 = f32[2,128,128]{1,2,0:T(8,128)S(1)} custom-call(f32[2,128,128]{2,1,0:T(8,128)S(1)} %get-tuple-element.44), custom_call_target="InvertDiagBlocksLowerTriangular" | custom-call | tf_op jit(solution)/shard_map/triangular_solve/custom-call.1 | solution.py:27
  372.5 10.7 broadcast_select_fusion.5
  383.3 175.6 %all-reduce.15.cloned.1.call-done = (f32[4096,256]{0,1:T(8,128)}, f32[4096,256]{0,1:T(8,128)}) async-done(((f32[4096,256]{0,1:T(8,128)}, f32[4096,256]{0,1:T(8,128)}), (f32[4096,256]{0,1:T(8,128)}, f32[4096,256]{0,1:T(8,128)})) %all-reduce.15.cloned.1.call-update) | async-done | bytes 8388624 | tf_op jit(solution)/shard_map/psum | solution.py:12
  559.0 7.0 reshape.187
  566.0 8.3 fusion.22
  583.2 8.3 fusion.21
  600.9 96.8 %all-reduce.21.cloned.1.call-done = (f32[2048,256]{0,1:T(8,128)}, f32[2048,256]{0,1:T(8,128)}) async-done(((f32[2048,256]{0,1:T(8,128)}, f32[2048,256]{0,1:T(8,128)}), (f32[2048,256]{0,1:T(8,128)}, f32[2048,256]{0,1:T(8,128)})) %all-reduce.21.cloned.1.call-update) | async-done | bytes 4194320 | tf_op jit(solution)/shard_map/psum | solution.py:81
  697.7 65.8 %fusion = f32[4096,2048]{0,1:T(8,128)} fusion(f32[4096,2048]{0,1:T(8,128)} %copy.36, s32[4096]{0:T(1024)S(1)} %bitcast.140, s32[2048]{0:T(1024)S(1)} %bitcast.138, f32[4096,256]{0,1:T(8,128)} %get-tuple-element.80, f32[4096,256]{0,1:T(8,128)} %get-tuple-element.81, f32[2048,256]{0,1:T(8,128)} %get-tuple-element.86, f32[2048,256]{0,1:T(8,128)} %get-tuple-element.87), kind=kOutput, calls=%fused_computation.8 | convolution fusion | flops 51567919104 | bytes 79716352 | tf_op jit(solution)/shard_map/dot_general | solution.py:20
  763.6 12.5 constant_dynamic-update-slice_fusion
  777.9 45.5 %all-reduce.19.cloned.1.call-done = (f32[256,256]{0,1:T(8,128)}, f32[256,256]{0,1:T(8,128)}) async-done(((f32[256,256]{0,1:T(8,128)}, f32[256,256]{0,1:T(8,128)}), (f32[256,256]{0,1:T(8,128)}, f32[256,256]{0,1:T(8,128)})) %all-reduce.19.cloned.1.call-update) | async-done | bytes 524304 | tf_op jit(solution)/shard_map/psum | solution.py:12
  832.7 19.7 %custom-call.9 = f32[2,128,128]{1,2,0:T(8,128)S(1)} custom-call(f32[2,128,128]{2,1,0:T(8,128)S(1)} %get-tuple-element.45), custom_call_target="InvertDiagBlocksLowerTriangular" | custom-call | tf_op jit(solution)/shard_map/triangular_solve/custom-call.1 | solution.py:27
  867.1 175.7 %all-reduce.13.cloned.1.call-done = (f32[4096,256]{0,1:T(8,128)}, f32[4096,256]{0,1:T(8,128)}) async-done(((f32[4096,256]{0,1:T(8,128)}, f32[4096,256]{0,1:T(8,128)}), (f32[4096,256]{0,1:T(8,128)}, f32[4096,256]{0,1:T(8,128)})) %all-reduce.13.cloned.1.call-update) | async-done | bytes 8388624 | tf_op jit(solution)/shard_map/psum | solution.py:12
  1049.5 8.3 fusion.24
  1066.8 8.3 fusion.23
  1083.7 97.5 %all-reduce.17.cloned.1.call-done = (f32[2048,256]{0,1:T(8,128)}, f32[2048,256]{0,1:T(8,128)}) async-done(((f32[2048,256]{0,1:T(8,128)}, f32[2048,256]{0,1:T(8,128)}), (f32[2048,256]{0,1:T(8,128)}, f32[2048,256]{0,1:T(8,128)})) %all-reduce.17.cloned.1.call-update) | async-done | bytes 4194320 | tf_op jit(solution)/shard_map/psum | solution.py:81
  1181.2 66.0 %fusion.1 = f32[4096,2048]{0,1:T(8,128)} fusion(f32[4096,2048]{0,1:T(8,128)} %get-tuple-element.90, s32[4096]{0:T(1024)S(1)} %bitcast.141, s32[2048]{0:T(1024)S(1)} %bitcast.139, f32[4096,256]{0,1:T(8,128)} %get-tuple-element.78, f32[4096,256]{0,1:T(8,128)} %get-tuple-element.79, f32[2048,256]{0,1:T(8,128)} %get-tuple-element.82, ...), kind=kOutput, calls=%fused_computation.9 | convolution fusion | flops 51567919104 | bytes 79716352 | tf_op jit(solution)/shard_map/dot_general | solution.py:20
  1253.9 30.1 %copy.52 = f32[256,8,16,256]{3,2,1,0:T(8,128)} copy(f32[256,8,16,256]{3,1,2,0:T(8,128)} %bitcast.117) | data formatting | bytes 67108864
  1284.0 48.7 %copy.30 = f32[16,1,256,8,1,256]{5,4,3,2,1,0:T(1,128)} copy(f32[16,1,256,8,1,256]{2,0,5,3,4,1:T(8,128)} %bitcast.121) | data formatting | bytes 67108864 | tf_op jit(solution)/shard_map/reshape | solution.py:97
  (116 shorter events, 120.4 us)
Async XLA Ops:
  6.5 329.5 %all-reduce.23.cloned.1.call-start = ((), (), s32[]{:S(2)}) async-start(), calls=%async_computation.5 | async-start | bytes 1048576 | tf_op jit(solution)/shard_map/psum | solution.py:12
  287.8 271.2 %all-reduce.15.cloned.1.call-start = ((), (), s32[]{:S(2)}) async-start(), calls=%async_computation.1 | async-start | bytes 16777216 | tf_op jit(solution)/shard_map/psum | solution.py:12
  336.0 27.2 %copy-start.6 = (f32[256,256]{0,1:T(8,128)S(1)}, f32[256,256]{0,1:T(8,128)}, u32[]{:S(2)}) copy-start(f32[256,256]{0,1:T(8,128)} %get-tuple-element.88) | copy-start | bytes 786436
  372.5 10.8 copy-start.2
  383.3 314.5 %all-reduce.21.cloned.1.call-start = ((), (), s32[]{:S(2)}) async-start(), calls=%async_computation.4 | async-start | bytes 8388608 | tf_op jit(solution)/shard_map/psum | solution.py:81
  593.8 229.6 %all-reduce.19.cloned.1.call-start = ((), (), s32[]{:S(2)}) async-start(), calls=%async_computation.3 | async-start | bytes 1048576 | tf_op jit(solution)/shard_map/psum | solution.py:12
  777.8 264.9 %all-reduce.13.cloned.1.call-start = ((), (), s32[]{:S(2)}) async-start(), calls=%async_computation | async-start | bytes 16777216 | tf_op jit(solution)/shard_map/psum | solution.py:12
  823.4 30.1 %copy-start.7 = (f32[256,256]{0,1:T(8,128)S(1)}, f32[256,256]{0,1:T(8,128)}, u32[]{:S(2)}) copy-start(f32[256,256]{0,1:T(8,128)} %get-tuple-element.84) | copy-start | bytes 786436
  854.4 6.1 copy-start.3
  860.5 6.5 copy-start
  867.0 314.2 %all-reduce.17.cloned.1.call-start = ((), (), s32[]{:S(2)}) async-start(), calls=%async_computation.2 | async-start | bytes 8388608 | tf_op jit(solution)/shard_map/psum | solution.py:81
  1181.2 66.0 %copy-start.1 = (f32[4096,256]{0,1:T(8,128)S(1)}, f32[4096,256]{0,1:T(8,128)}, u32[]{:S(2)}) copy-start(f32[4096,256]{0,1:T(8,128)} %copy-done) | copy-start | bytes 12582916
  1181.2 66.0 %copy-start.4 = (f32[32,8,16,256]{3,1,2,0:T(8,128)S(1)}, f32[32,8,16,256]{3,1,2,0:T(8,128)}, u32[]{:S(2)}) copy-start(f32[32,8,16,256]{3,1,2,0:T(8,128)} %copy.51) | copy-start | bytes 12582916
  1181.2 66.0 %copy-start.5 = (f32[4096,256]{0,1:T(8,128)S(1)}, f32[4096,256]{0,1:T(8,128)}, u32[]{:S(2)}) copy-start(f32[4096,256]{0,1:T(8,128)} %get-tuple-element.103) | copy-start | bytes 12582916
Sparse Core Ops, SparseCore 0:
  287.9 48.1 all-reduce.22
  383.4 175.5 all-reduce.14
  593.9 103.7 all-reduce.20
  777.9 45.4 all-reduce.18
  867.1 175.5 all-reduce.12
  1077.4 103.7 all-reduce.16
where the time goes:
time: 1350 us; the launch traced here: 1340 us
  waiting for transfers between devices  622 us (46%)
  other arithmetic  292 us (22%)
  local copies, waits for them, and re-layouts  246 us (18%)
  matrix products  165 us (12%)
  between operations  14.1 us (1%)
    psum x4, waiting for transfers between devices, spread(): return lax.psum(block, axis)  428 us
    psum x2, waiting for transfers between devices, on_device(): lax.psum((jnp.where(keeper, select_columns(got_half), 0.0), jnp.where(kee...  194 us
    unnamed x4, other arithmetic  187 us
    dot_general x6, matrix products, product_trans(): lax.dot_general(left, right, (((1,), (1,)), ((), ())), precision=highest,...  150 us
    unnamed x29, local copies, waits for them, and re-layouts  117 us
    reshape x1, local copies, waits for them, and re-layouts, on_device(): return local.reshape(row_tiles, 1, width, col_tiles, 1, width)  48.7 us
    another operation x5, other arithmetic, diagonal_core(): lax.linalg.triangular_solve(diag_factor, identity, left_side=True, lower=...  41.3 us
    reshape x1, local copies, waits for them, and re-layouts, on_device(): local = matrix.reshape(height, col_tiles * width)  31.1 us
  transfers between devices with their start and end apart: 6, of which 6 were waited for; matrix products, arithmetic and copies ran while one was open for 2% of the time, Pallas kernels for 0%

commit v1 on v0

--- a/solution.py
+++ b/solution.py
@@ -9,7 +9,7 @@
 
 def spread(block, axis, source):
     block = jnp.where(lax.axis_index(axis) == source, block, jnp.zeros_like(block))
-    return lax.psum(block, axis)
+    return jnp.sum(lax.all_gather(block, axis), axis=0)
 
 
 def product(left, right):

time: 1350 us -> 1950 us (1.44)
  waiting for transfers between devices: 622 us -> 1240 us
  other arithmetic: 292 us -> 353 us
  local copies, waits for them, and re-layouts: 246 us -> 185 us
    all_gather x0 -> x8, waiting for transfers between devices: none -> 1030 us  [spread(): return jnp.sum(lax.all_gather(block, axis), axis=0)]
    psum x4 -> x0, waiting for transfers between devices: 428 us -> none  [spread(): return lax.psum(block, axis)]
    reduce_sum x0 -> x8, other arithmetic: none -> 68.2 us  [spread(): return jnp.sum(lax.all_gather(block, axis), axis=0)]
    reshape x1 -> x0, local copies, waits for them, and re-layouts: 31.1 us -> none  [on_device(): local = matrix.reshape(height, col_tiles * width)]
    unnamed x29 -> x34, local copies, waits for them, and re-layouts: 117 us -> 96.1 us
  transfers between devices with their start and end apart: 6 -> 10, of which waited for: 6 -> 8; matrix products, arithmetic and copies ran while one was open for 2% -> 19% of each run, Pallas kernels for 0% -> 0%
where the time goes in v1:
time: 1950 us
  waiting for transfers between devices  1240 us (64%)
  other arithmetic  353 us (18%)
  local copies, waits for them, and re-layouts  185 us (9%)
  matrix products  156 us (8%)
    all_gather x8, waiting for transfers between devices, spread(): return jnp.sum(lax.all_gather(block, axis), axis=0)  1030 us
    psum x2, waiting for transfers between devices, on_device(): lax.psum((jnp.where(keeper, select_columns(got_half), 0.0), jnp.where(kee...  202 us
    unnamed x4, other arithmetic  188 us
    dot_general x6, matrix products, product_trans(): lax.dot_general(left, right, (((1,), (1,)), ((), ())), precision=highest,...  141 us
    unnamed x34, local copies, waits for them, and re-layouts  96.1 us
    reduce_sum x8, other arithmetic, spread(): return jnp.sum(lax.all_gather(block, axis), axis=0)  68.2 us
    reshape x1, local copies, waits for them, and re-layouts, on_device(): return local.reshape(row_tiles, 1, width, col_tiles, 1, width)  48.3 us
    another operation x5, other arithmetic, diagonal_core(): lax.linalg.triangular_solve(diag_factor, identity, left_side=True, lower=...  39.4 us
  transfers between devices with their start and end apart: 10, of which 8 were waited for; matrix products, arithmetic and copies ran while one was open for 19% of the time, Pallas kernels for 0%

profile of v1, /device:TPU:0, one launch (start us, length us, event | category | flops | bytes accessed | tf_op | source)
XLA Modules:
  0.0 1946.5 jit_solution(5426693124989677940)
XLA Ops:
  6.5 93.9 %reduce.10 = f32[16,256,8,256]{3,2,1,0:T(8,128)} reduce(f32[16,1,256,8,1,256]{5,4,3,2,1,0:T(1,128)} %param.8, f32[]{:T(128)} %constant.182), dimensions={1,4}, to_apply=%param.8.reduce_sub_computation | reduce | bytes 67108864 | tf_op args[0]
  100.4 29.9 %copy.72 = f32[512,8,8,256]{3,1,2,0:T(8,128)} copy(f32[512,8,8,256]{3,2,1,0:T(8,128)} %bitcast.122) | data formatting | bytes 67108864
  132.7 93.9 %reduce.9 = f32[16,256,8,256]{3,2,1,0:T(8,128)} reduce(f32[16,1,256,8,1,256]{5,4,3,2,1,0:T(1,128)} %param.9, f32[]{:T(128)} %constant.182), dimensions={1,4}, to_apply=%param.9.reduce_sub_computation | reduce | bytes 67108864 | tf_op args[1]
  226.6 19.9 %copy.75 = f32[512,8,8,256]{3,1,2,0:T(8,128)S(1)} copy(f32[512,8,8,256]{3,2,1,0:T(8,128)} %bitcast.121) | data formatting | bytes 67108864
  246.5 11.7 copy-done
  268.7 19.8 %all-gather.17.cloned.1.call-done = f32[1024,256]{1,0:T(8,128)} async-done(((f32[256,256]{1,0:T(8,128)}), f32[1024,256]{1,0:T(8,128)}) %all-gather.17.cloned.1.call-update) | async-done | bytes 1048592 | tf_op jit(solution)/shard_map/all_gather | solution.py:12
  294.3 19.7 %custom-call.8 = f32[2,128,128]{1,2,0:T(8,128)S(1)} custom-call(f32[2,128,128]{2,1,0:T(8,128)S(1)} %get-tuple-element.44), custom_call_target="InvertDiagBlocksLowerTriangular" | custom-call | tf_op jit(solution)/shard_map/triangular_solve/custom-call.1 | solution.py:27
  324.6 9.1 broadcast_select_fusion.5
  334.1 245.0 %all-gather.23.cloned.1.call-done = f32[32768,256]{1,0:T(8,128)} async-done(((f32[4096,256]{1,0:T(8,128)}), f32[32768,256]{1,0:T(8,128)}) %all-gather.23.cloned.1.call-update) | async-done | bytes 33554448 | tf_op jit(solution)/shard_map/all_gather | solution.py:12
  579.1 16.9 reduce_sum.75
  608.5 8.3 fusion.21
  619.0 248.1 %all-gather.21.cloned.1.call-done = f32[32768,256]{1,0:T(8,128)} async-done(((f32[4096,256]{1,0:T(8,128)}), f32[32768,256]{1,0:T(8,128)}) %all-gather.21.cloned.1.call-update) | async-done | bytes 33554448 | tf_op jit(solution)/shard_map/all_gather | solution.py:12
  867.1 14.4 reduce_sum.74
  906.6 99.9 %all-reduce.7.cloned.1.call-done = (f32[2048,256]{0,1:T(8,128)}, f32[2048,256]{0,1:T(8,128)}) async-done(((f32[2048,256]{0,1:T(8,128)}, f32[2048,256]{0,1:T(8,128)}), (f32[2048,256]{0,1:T(8,128)}, f32[2048,256]{0,1:T(8,128)})) %all-reduce.7.cloned.1.call-update) | async-done | bytes 4194320 | tf_op jit(solution)/shard_map/psum | solution.py:81
  1006.4 62.0 %fusion = f32[4096,2048]{1,0:T(8,128)} fusion(f32[4096,2048]{1,0:T(8,128)} %bitcast.120, s32[2048]{0:T(1024)S(1)} %bitcast.145, s32[4096]{0:T(1024)S(1)} %bitcast.147, f32[4096,256]{0,1:T(8,128)} %copy.68, f32[4096,256]{0,1:T(8,128)} %copy.67, f32[2048,256]{0,1:T(8,128)} %get-tuple-element.80, f32[2048,256]{0,1:T(8,128)} %get-tuple-element.81), kind=kOutput, calls=%fused_computation.8 | convolution fusion | flops 51567919104 | bytes 79716352 | tf_op jit(solution)/shard_map/dot_general | solution.py:20
  1083.7 19.7 %custom-call.9 = f32[2,128,128]{1,2,0:T(8,128)S(1)} custom-call(f32[2,128,128]{2,1,0:T(8,128)S(1)} %get-tuple-element.45), custom_call_target="InvertDiagBlocksLowerTriangular" | custom-call | tf_op jit(solution)/shard_map/triangular_solve/custom-call.1 | solution.py:27
  1122.8 271.9 %all-gather.31.cloned.1.call-done = f32[32768,256]{1,0:T(8,128)} async-done(((f32[4096,256]{1,0:T(8,128)}), f32[32768,256]{1,0:T(8,128)}) %all-gather.31.cloned.1.call-update) | async-done | bytes 33554448 | tf_op jit(solution)/shard_map/all_gather | solution.py:12
  1394.7 17.3 reduce_sum.79
  1424.5 8.3 fusion.23
  1435.1 248.1 %all-gather.29.cloned.1.call-done = f32[32768,256]{1,0:T(8,128)} async-done(((f32[4096,256]{1,0:T(8,128)}), f32[32768,256]{1,0:T(8,128)}) %all-gather.29.cloned.1.call-update) | async-done | bytes 33554448 | tf_op jit(solution)/shard_map/all_gather | solution.py:12
  1683.2 14.3 reduce_sum.78
  1720.6 101.8 %all-reduce.5.cloned.1.call-done = (f32[2048,256]{0,1:T(8,128)}, f32[2048,256]{0,1:T(8,128)}) async-done(((f32[2048,256]{0,1:T(8,128)}, f32[2048,256]{0,1:T(8,128)}), (f32[2048,256]{0,1:T(8,128)}, f32[2048,256]{0,1:T(8,128)})) %all-reduce.5.cloned.1.call-update) | async-done | bytes 4194320 | tf_op jit(solution)/shard_map/psum | solution.py:81
  1822.5 62.3 %fusion.1 = f32[4096,2048]{1,0:T(8,128)} fusion(f32[4096,2048]{1,0:T(8,128)} %get-tuple-element.92, s32[2048]{0:T(1024)S(1)} %bitcast.146, s32[4096]{0:T(1024)S(1)} %bitcast.148, f32[4096,256]{0,1:T(8,128)} %copy.71, f32[4096,256]{0,1:T(8,128)} %copy.70, f32[2048,256]{0,1:T(8,128)} %get-tuple-element.78, f32[2048,256]{0,1:T(8,128)} %get-tuple-element.79), kind=kOutput, calls=%fused_computation.9 | convolution fusion | flops 51567919104 | bytes 79716352 | tf_op jit(solution)/shard_map/dot_general | solution.py:20
  1890.8 48.3 %reshape.239 = f32[16,1,256,8,1,256]{5,4,3,2,1,0:T(1,128)} reshape(f32[4096,2048]{1,0:T(8,128)} %fusion.11) | data formatting | bytes 67108864 | tf_op jit(solution)/shard_map/reshape | solution.py:97
  (135 shorter events, 155.7 us)
Async XLA Ops:
  6.5 260.6 %all-gather.19.cloned.1.call-start = ((), (), s32[]{:S(2)}) async-start(), calls=%async_computation.1 | async-start | bytes 1310720 | tf_op jit(solution)/shard_map/all_gather | solution.py:12
  132.1 156.3 %all-gather.17.cloned.1.call-start = ((), (), s32[]{:S(2)}) async-start(), calls=%async_computation | async-start | bytes 1310720 | tf_op jit(solution)/shard_map/all_gather | solution.py:12
  246.5 11.7 copy-start
  259.1 320.0 %all-gather.23.cloned.1.call-start = ((), (), s32[]{:S(2)}) async-start(), calls=%async_computation.3 | async-start | bytes 37748736 | tf_op jit(solution)/shard_map/all_gather | solution.py:12
  266.9 600.2 %all-gather.21.cloned.1.call-start = ((), (), s32[]{:S(2)}) async-start(), calls=%async_computation.2 | async-start | bytes 37748736 | tf_op jit(solution)/shard_map/all_gather | solution.py:12
  324.6 9.2 copy-start.1
  333.8 672.6 %all-reduce.7.cloned.1.call-start = ((), (), s32[]{:S(2)}) async-start(), calls=%async_computation.9 | async-start | bytes 8388608 | tf_op jit(solution)/shard_map/psum | solution.py:81
  904.5 173.5 %all-gather.25.cloned.1.call-start = ((), (), s32[]{:S(2)}) async-start(), calls=%async_computation.4 | async-start | bytes 1310720 | tf_op jit(solution)/shard_map/all_gather | solution.py:12
  905.0 199.5 %all-gather.27.cloned.1.call-start = ((), (), s32[]{:S(2)}) async-start(), calls=%async_computation.5 | async-start | bytes 1310720 | tf_op jit(solution)/shard_map/all_gather | solution.py:12
  1006.4 62.0 %copy-start.2 = (f32[4096,256]{1,0:T(8,128)S(1)}, f32[4096,256]{1,0:T(8,128)}, u32[]{:S(2)}) copy-start(f32[4096,256]{1,0:T(8,128)} %copy-done.1) | copy-start | bytes 12582916
  1006.4 62.0 %copy-start.7 = (f32[4096,256]{1,0:T(8,128)S(1)}, f32[4096,256]{1,0:T(8,128)}, u32[]{:S(2)}) copy-start(f32[4096,256]{1,0:T(8,128)} %get-tuple-element.91) | copy-start | bytes 12582916
  1074.4 2.0 copy-start.5
  1077.2 317.6 %all-gather.31.cloned.1.call-start = ((), (), s32[]{:S(2)}) async-start(), calls=%async_computation.7 | async-start | bytes 37748736 | tf_op jit(solution)/shard_map/all_gather | solution.py:12
  1077.9 605.3 %all-gather.29.cloned.1.call-start = ((), (), s32[]{:S(2)}) async-start(), calls=%async_computation.6 | async-start | bytes 37748736 | tf_op jit(solution)/shard_map/all_gather | solution.py:12
  1109.4 6.5 copy-start.6
  1115.9 6.9 copy-start.3
  1122.8 699.7 %all-reduce.5.cloned.1.call-start = ((), (), s32[]{:S(2)}) async-start(), calls=%async_computation.8 | async-start | bytes 8388608 | tf_op jit(solution)/shard_map/psum | solution.py:81
  1822.5 62.3 %copy-start.4 = (f32[4096,256]{1,0:T(8,128)S(1)}, f32[4096,256]{1,0:T(8,128)}, u32[]{:S(2)}) copy-start(f32[4096,256]{1,0:T(8,128)} %copy-done.3) | copy-start | bytes 12582916
  1822.5 62.3 %copy-start.8 = (f32[4096,256]{1,0:T(8,128)S(1)}, f32[4096,256]{1,0:T(8,128)}, u32[]{:S(2)}) copy-start(f32[4096,256]{1,0:T(8,128)} %get-tuple-element.95) | copy-start | bytes 12582916
Sparse Core Ops, SparseCore 0:
  132.2 29.2 all-gather.18
  259.2 29.2 all-gather.16
  290.0 289.0 all-gather.22
  580.5 286.5 all-gather.20
  904.6 101.8 all-reduce.6
  1008.1 26.4 all-gather.24
  1077.3 27.1 all-gather.26
  1106.1 288.5 all-gather.30
  1396.4 286.7 all-gather.28
  1720.6 101.8 all-reduce.4
